TPU v7x, 32 devices: a whole 2x2x4 slice. The times are simulated.
32 devices in a mesh: expert: 16 (over z, y, core), tensor: 2 (over x).
Axes of the slice: x: 2, y: 2, z: 4, core: 2. Of those that a mesh axis runs over, the one named last changes fastest.
Arguments:
- tokens: bfloat16 [64, 256, 1280], P(('expert', 'tensor')), may hold values from -6 to 6
- slot_keys: bfloat16 [1280, 16], replicated, may hold values from -6 to 6
- logit_scale: float32 [], replicated, may hold values from 40 to 80
- w_in: bfloat16 [16, 1280, 3584], P('expert', None, 'tensor'), may hold values from -0.625 to 0.625
- b_in: bfloat16 [16, 3584], P('expert', 'tensor'), may hold values from -3 to 3
- w_out: bfloat16 [16, 3584, 1280], P('expert', 'tensor'), may hold values from -0.09375 to 0.09375
- b_out: bfloat16 [16, 1280], P('expert'), may hold values from -3 to 3
Outputs:
- mixed: bfloat16 [64, 256, 1280], P(('expert', 'tensor'))
All inputs are finite; a program needn't handle non-finite values.
Results may differ from a plain program's by a relative error of at most 0.0071.
Values may be sent and summed in bfloat16 or wider, within the bound.
A program may use at most 64 MiB of HBM per device.

v0:
```python
import jax
import jax.numpy as jnp
from jax import lax
from jax.sharding import PartitionSpec as P

EPS = 1e-06


def local(tokens, slot_keys, logit_scale, w_in, b_in, w_out, b_out):
    images, seq_len, width = tokens.shape
    slots = slot_keys.shape[1]
    row_sq = jnp.sum(jnp.square(tokens.astype(jnp.float32)), axis=2, keepdims=True)
    row_inv = lax.rsqrt(row_sq + EPS)
    key_sq = jnp.sum(jnp.square(slot_keys.astype(jnp.float32)), axis=0)
    key_inv = lax.rsqrt(key_sq + EPS)
    raw = jnp.dot(
        tokens.reshape(images * seq_len, width), slot_keys, preferred_element_type=jnp.float32
    )
    logits = logit_scale * row_inv * key_inv * raw.reshape(images, seq_len, slots)
    expo = jnp.exp(logits)
    dispatch = (expo / jnp.sum(expo, axis=1, keepdims=True)).astype(jnp.bfloat16)
    combine = (expo / jnp.sum(expo, axis=2, keepdims=True)).astype(jnp.bfloat16)
    slot_in = jnp.einsum(
        "ims,imd->isd", dispatch, tokens, preferred_element_type=jnp.float32
    ).astype(jnp.bfloat16)
    routed = lax.all_to_all(slot_in, "expert", split_axis=1, concat_axis=0, tiled=True)
    bias_wide = b_in.astype(jnp.float32)
    pre = (
        jnp.einsum(
            "rkd,kdf->rkf",
            lax.all_gather(routed, "tensor", axis=0, tiled=True),
            w_in,
            preferred_element_type=jnp.float32,
        )
        + bias_wide[None]
    )
    hidden = jax.nn.gelu(pre).astype(jnp.bfloat16)
    mine = lax.psum_scatter(
        jnp.einsum("rkf,kfd->rkd", hidden, w_out, preferred_element_type=jnp.float32),
        "tensor",
        scatter_dimension=0,
        tiled=True,
    )
    slot_out = (mine + b_out.astype(jnp.float32)[None]).astype(jnp.bfloat16)
    returned = lax.all_to_all(slot_out, "expert", split_axis=0, concat_axis=1, tiled=True)
    mixed = jnp.einsum("ims,isd->imd", combine, returned, preferred_element_type=jnp.float32)
    return mixed.astype(jnp.bfloat16)


def solution(mesh):
    placed = (
        P(("expert", "tensor"), None, None),
        P(),
        P(),
        P("expert", None, "tensor"),
        P("expert", "tensor"),
        P("expert", "tensor", None),
        P("expert", None),
    )
    return jax.shard_map(
        local,
        mesh=mesh,
        in_specs=placed,
        out_specs=P(("expert", "tensor"), None, None),
        check_vma=False,
    )
```

profile of v0, /device:TPU:0, one launch (start us, length us, event | category | flops | bytes accessed | tf_op | source)
XLA Modules:
  0.0 72.5 jit_solution(5864950734486424679)
XLA Ops:
  6.5 0.0 copy-start
  6.5 0.0 copy-start.1
  7.3 0.9 %multiply_reduce_fusion.1 = f32[16]{0:T(128)S(1)} fusion(bf16[1280,16]{0,1:T(8,128)(2,1)} %param.8), kind=kLoop, calls=%fused_computation.32 | loop fusion | flops 61424 | bytes 41024 | tf_op jit(solution)/shard_map/reduce_sum | solution.py:14
  8.2 1.7 %multiply_reduce_fusion = f32[2,256]{1,0:T(2,128)S(1)} fusion(bf16[2,256,1280]{2,1,0:T(8,128)(2,1)} %param.7), kind=kLoop, calls=%fused_computation.5 | loop fusion | flops 1965568 | bytes 1312768 | tf_op jit(solution)/shard_map/reduce_sum | solution.py:12
  9.9 1.8 %fusion.16 = f32[2,256,16]{1,2,0:T(8,128)S(1)} fusion(bf16[2,256,1280]{2,1,0:T(8,128)(2,1)} %param.7, bf16[1280,16]{0,1:T(8,128)(2,1)} %param.8, f32[16]{0:T(128)S(1)} %add_rsqrt_fusion, f32[2,256]{1,0:T(2,128)S(1)} %rsqrt_multiply_fusion), kind=kOutput, calls=%fused_computation.12 | convolution fusion | flops 20987904 | bytes 1386560 | tf_op jit(solution)/shard_map/dot_general | solution.py:16
  11.7 0.0 copy-done
  11.7 0.3 convolution_convert_fusion.1
  12.0 0.7 copy.13
  12.7 7.4 %all-to-all-start = ((bf16[2,16,1280]{2,0,1:T(2,128)(2,1)}), bf16[2,16,1280]{2,0,1:T(2,128)(2,1)S(1)}, u32[]{:S(2)}, u32[]{:S(2)}) async-start(bf16[2,16,1280]{2,0,1:T(2,128)(2,1)} %copy.13), calls=%async_computation | async-start | bytes 163840 | tf_op jit(solution)/shard_map/all_to_all | solution.py:26
  20.1 0.0 reduce-scatter.2.cloned.1.call-start
  20.2 0.0 copy-done.1
  20.2 7.0 %all-to-all-done = bf16[2,16,1280]{2,0,1:T(2,128)(2,1)S(1)} async-done(((bf16[2,16,1280]{2,0,1:T(2,128)(2,1)}), bf16[2,16,1280]{2,0,1:T(2,128)(2,1)S(1)}, u32[]{:S(2)}, u32[]{:S(2)}) %all-to-all-start) | async-done | bytes 81952 | tf_op jit(solution)/shard_map/all_to_all | solution.py:26
  27.3 5.1 %all_gather.3 = bf16[64,1,1280]{2,0,1:T(8,128)(2,1)S(1)} all-gather(bf16[32,1,1280]{2,0,1:T(8,128)(2,1)S(1)} %all_to_all.29), channel_id=1, replica_groups=mesh['expert'=16,'tensor'=2] {'tensor'}, dimensions={0}, use_global_device_ids=true | all-gather | bytes 245760 | tf_op jit(solution)/shard_map/all_gather | solution.py:31
  32.4 0.0 copy-start.2
  32.4 6.3 %fusion.4 = f32[64,1,1280]{2,0,1:T(8,128)} fusion(bf16[1,1792,1280]{2,1,0:T(8,128)(2,1)} %param.12, bf16[1,1280,1792]{2,1,0:T(8,128)(2,1)} %param.10, f32[1792]{0:T(1024)S(1)} %convert_reduce_fusion, bf16[64,1,1280]{2,0,1:T(8,128)(2,1)S(1)} %all_gather.3), kind=kOutput, calls=%fused_computation.6 | convolution fusion | flops 588349440 | bytes 9673728 | tf_op jit(solution)/shard_map/rkf,kfd->rkd/dot_general | solution.py:39
  38.7 0.0 reduce-scatter.2.cloned.1.call-update
  38.7 0.0 copy-done.2
  38.7 10.0 %reduce-scatter.2.cloned.1.call-done = f32[32,1,1280]{2,0,1:T(8,128)} async-done(((f32[64,1,1280]{2,0,1:T(8,128)}), f32[32,1,1280]{2,0,1:T(8,128)}) %reduce-scatter.2.cloned.1.call-update) | async-done | bytes 163856 | tf_op jit(solution)/shard_map/reduce_scatter | solution.py:38
  48.7 0.9 %add_convert_fusion = bf16[32,1,1280]{2,0,1:T(8,128)(2,1)S(1)} fusion(f32[32,1,1280]{2,0,1:T(8,128)} %reduce-scatter.2.cloned.1.call-done, f32[1280]{0:T(1024)S(1)} %convert_reduce_fusion.1), kind=kLoop, calls=%fused_computation.29 | loop fusion | flops 81920 | bytes 250880 | tf_op jit(solution)/shard_map/convert_element_type | solution.py:44
  49.7 0.5 broadcast.27
  50.2 0.7 reduce.5
  50.9 12.5 %all_to_all.36 = bf16[16,2,1280]{2,1,0:T(2,128)(2,1)S(1)} all-to-all(bf16[16,2,1280]{2,1,0:T(2,128)(2,1)S(1)} %reshape.50), channel_id=1, replica_groups=mesh['expert'=16,'tensor'=2] {'expert'}, dimensions={0} | all-to-all | bytes 163840 | tf_op jit(solution)/shard_map/all_to_all | solution.py:45
  63.4 0.1 reshape.51
  63.5 0.5 reduce.2
  64.0 1.6 %convolution_convert_fusion = bf16[2,256,1280]{2,1,0:T(8,128)(2,1)} fusion(bf16[16,2,1,1280]{3,1,0,2:T(2,128)(2,1)S(1)} %all_to_all.31, f32[2,256,16]{1,2,0:T(8,128)S(1)} %fusion.16), kind=kOutput, calls=%fused_computation.4 | convolution fusion | flops 21643792 | bytes 1425408 | tf_op jit(solution)/shard_map/ims,isd->imd/dot_general | solution.py:46
  (7 shorter events, 0.2 us)
Async XLA Ops:
  6.5 5.1 %copy-start = (bf16[2,256,1280]{2,1,0:T(8,128)(2,1)S(1)}, bf16[2,256,1280]{2,1,0:T(8,128)(2,1)}, u32[]{:S(2)}) copy-start(bf16[2,256,1280]{2,1,0:T(8,128)(2,1)} %param.7) | copy-start | bytes 3932164
  6.5 13.6 %copy-start.1 = (bf16[1,1792]{1,0:T(2,128)(2,1)S(1)}, bf16[1,1792]{1,0:T(2,128)(2,1)}, u32[]{:S(2)}) copy-start(bf16[1,1792]{1,0:T(2,128)(2,1)} %param.11) | copy-start | bytes 10756
  12.7 14.5 %all-to-all-start = ((bf16[2,16,1280]{2,0,1:T(2,128)(2,1)}), bf16[2,16,1280]{2,0,1:T(2,128)(2,1)S(1)}, u32[]{:S(2)}, u32[]{:S(2)}) async-start(bf16[2,16,1280]{2,0,1:T(2,128)(2,1)} %copy.13), calls=%async_computation | async-start | bytes 163840 | tf_op jit(solution)/shard_map/all_to_all | solution.py:26
  20.1 28.6 %reduce-scatter.2.cloned.1.call-start = ((), (), s32[]{:S(2)}) async-start(), calls=%async_computation.3 | async-start | bytes 491520 | tf_op jit(solution)/shard_map/reduce_scatter | solution.py:38
  32.4 6.3 %copy-start.2 = (bf16[1,1280]{1,0:T(2,128)(2,1)S(1)}, bf16[1,1280]{1,0:T(2,128)(2,1)}, u32[]{:S(2)}) copy-start(bf16[1,1280]{1,0:T(2,128)(2,1)} %param.13) | copy-start | bytes 7684
Sparse Core Ops, SparseCore 0:
  38.8 9.8 reduce-scatter.1
where the time goes:
time: 72.8 us; the launch traced here: 72.5 us
  blocking collectives  17.6 us (24%)
  waiting for transfers between devices  17.1 us (23%)
  between operations  14.3 us (20%)
  matrix products  9.99 us (14%)
  starting transfers between devices  7.46 us (10%)
  other arithmetic  4.67 us (6%)
  local copies, waits for them, and re-layouts  1.4 us (2%)
    all_to_all x1, blocking collectives, local(): lax.all_to_all(slot_out, 'expert', split_axis=0, concat_axis=1, tiled=True)  12.5 us
    reduce_scatter x1, waiting for transfers between devices, local(): lax.psum_scatter(jnp.einsum('rkf,kfd->rkd', hidden, w_out, preferred_elem...  10 us
    all_to_all x1, starting transfers between devices, local(): lax.all_to_all(slot_in, 'expert', split_axis=1, concat_axis=0, tiled=True)  7.41 us
    all_to_all x1, waiting for transfers between devices, local(): lax.all_to_all(slot_in, 'expert', split_axis=1, concat_axis=0, tiled=True)  7.02 us
    dot_general x1, matrix products, local(): jnp.einsum('rkf,kfd->rkd', hidden, w_out, preferred_element_type=jnp.floa...  6.26 us
    all_gather x1, blocking collectives, local(): lax.all_gather(routed, 'tensor', axis=0, tiled=True)  5.11 us
    dot_general x1, matrix products, local(): jnp.dot(tokens.reshape(images * seq_len, width), slot_keys, preferred_ele...  1.78 us
    reduce_sum x1, other arithmetic, local(): jnp.sum(jnp.square(tokens.astype(jnp.float32)), axis=2, keepdims=True)  1.65 us
  transfers between devices with their start and end apart: 2, of which 2 were waited for; matrix products, arithmetic and copies ran while one was open for 0% of the time, Pallas kernels for 0%

commit v1 on v0

--- a/solution.py
+++ b/solution.py
@@ -4,6 +4,21 @@
 from jax.sharding import PartitionSpec as P
 
 EPS = 1e-06
+
+
+def ring_apply(shard, axis, dim, make, out_dim):
+    ways, here, step = (lax.axis_size(axis), lax.axis_index(axis), shard.shape[dim])
+    results = []
+    for far in range(ways):
+        arriving = (
+            lax.ppermute(shard, axis, [(d, (d + 1) % ways) for d in range(ways)])
+            if far + 1 < ways
+            else shard
+        )
+        results.append(make(shard, (here - far) % ways * step))
+        shard = arriving
+    line = jnp.concatenate(results[::-1], axis=out_dim)
+    return jnp.roll(line, (here + 1) * results[0].shape[out_dim], axis=out_dim)
 
 
 def local(tokens, slot_keys, logit_scale, w_in, b_in, w_out, b_out):
@@ -26,11 +41,14 @@
     routed = lax.all_to_all(slot_in, "expert", split_axis=1, concat_axis=0, tiled=True)
     bias_wide = b_in.astype(jnp.float32)
     pre = (
-        jnp.einsum(
-            "rkd,kdf->rkf",
-            lax.all_gather(routed, "tensor", axis=0, tiled=True),
-            w_in,
-            preferred_element_type=jnp.float32,
+        ring_apply(
+            routed,
+            "tensor",
+            0,
+            lambda part, start: jnp.einsum(
+                "rkd,kdf->rkf", part, w_in, preferred_element_type=jnp.float32
+            ),
+            0,
         )
         + bias_wide[None]
     )

time: 72.8 us -> 69.7 us (0.957)
  blocking collectives: 17.6 us -> 12.5 us
  starting transfers between devices: 7.46 us -> 9.01 us
  local copies, waits for them, and re-layouts: 1.4 us -> 2.82 us
    all_gather x1 -> x0, blocking collectives: 5.11 us -> none  [local(): lax.all_gather(routed, 'tensor', axis=0, tiled=True)]
    dot_general x1, matrix products: 6.26 us -> 1.76 us  [local(): jnp.einsum('rkf,kfd->rkd', hidden, w_out, preferred_element_type=jnp.floa...]
    dot_general x0 -> x2, matrix products: none -> 4.11 us  [local(): jnp.einsum('rkd,kdf->rkf', part, w_in, preferred_element_type=jnp.float32)]
    ppermute x0 -> x1, starting transfers between devices: none -> 1.56 us  [ring_apply(): lax.ppermute(shard, axis, [(d, (d + 1) % ways) for d in range(ways)])]
    unnamed x8 -> x12, local copies, waits for them, and re-layouts: 0.11 us -> 1.49 us
  transfers between devices with their start and end apart: 2 -> 3, of which waited for: 2 -> 2; matrix products, arithmetic and copies ran while one was open for 0% -> 5% of each run, Pallas kernels for 0% -> 0%
where the time goes in v1:
time: 69.7 us; the launch traced here: 69.3 us
  waiting for transfers between devices  16.4 us (24%)
  between operations  14.3 us (21%)
  blocking collectives  12.5 us (18%)
  matrix products  9.59 us (14%)
  starting transfers between devices  9.01 us (13%)
  other arithmetic  4.67 us (7%)
  local copies, waits for them, and re-layouts  2.82 us (4%)
    all_to_all x1, blocking collectives, local(): lax.all_to_all(slot_out, 'expert', split_axis=0, concat_axis=1, tiled=True)  12.5 us
    reduce_scatter x1, waiting for transfers between devices, local(): lax.psum_scatter(jnp.einsum('rkf,kfd->rkd', hidden, w_out, preferred_elem...  9.35 us
    all_to_all x1, starting transfers between devices, local(): lax.all_to_all(slot_in, 'expert', split_axis=1, concat_axis=0, tiled=True)  7.41 us
    all_to_all x1, waiting for transfers between devices, local(): lax.all_to_all(slot_in, 'expert', split_axis=1, concat_axis=0, tiled=True)  7 us
    dot_general x2, matrix products, local(): jnp.einsum('rkd,kdf->rkf', part, w_in, preferred_element_type=jnp.float32)  4.11 us
    dot_general x1, matrix products, local(): jnp.dot(tokens.reshape(images * seq_len, width), slot_keys, preferred_ele...  1.78 us
    dot_general x1, matrix products, local(): jnp.einsum('rkf,kfd->rkd', hidden, w_out, preferred_element_type=jnp.floa...  1.76 us
    reduce_sum x1, other arithmetic, local(): jnp.sum(jnp.square(tokens.astype(jnp.float32)), axis=2, keepdims=True)  1.65 us
  transfers between devices with their start and end apart: 3, of which 2 were waited for; matrix products, arithmetic and copies ran while one was open for 5% of the time, Pallas kernels for 0%

profile of v1, /device:TPU:0, one launch (start us, length us, event | category | flops | bytes accessed | tf_op | source)
XLA Modules:
  0.0 69.3 jit_solution(7838184708127693751)
XLA Ops:
  6.5 0.0 copy-start.1
  6.5 0.0 copy-start.2
  7.3 0.9 %multiply_reduce_fusion.1 = f32[16]{0:T(128)S(1)} fusion(bf16[1280,16]{0,1:T(8,128)(2,1)} %param.8), kind=kLoop, calls=%fused_computation.40 | loop fusion | flops 61424 | bytes 41024 | tf_op jit(solution)/shard_map/reduce_sum | solution.py:29
  8.2 1.7 %multiply_reduce_fusion = f32[2,256]{1,0:T(2,128)S(1)} fusion(bf16[2,256,1280]{2,1,0:T(8,128)(2,1)} %param.7), kind=kLoop, calls=%fused_computation.7 | loop fusion | flops 1965568 | bytes 1312768 | tf_op jit(solution)/shard_map/reduce_sum | solution.py:27
  9.9 1.8 %fusion.15 = f32[2,256,16]{1,2,0:T(8,128)S(1)} fusion(bf16[2,256,1280]{2,1,0:T(8,128)(2,1)} %param.7, bf16[1280,16]{0,1:T(8,128)(2,1)} %param.8, f32[16]{0:T(128)S(1)} %add_rsqrt_fusion, f32[2,256]{1,0:T(2,128)S(1)} %rsqrt_multiply_fusion), kind=kOutput, calls=%fused_computation.13 | convolution fusion | flops 20987904 | bytes 1386560 | tf_op jit(solution)/shard_map/dot_general | solution.py:31
  11.7 0.0 copy-done.1
  11.7 0.3 convolution_convert_fusion.1
  12.0 0.7 %copy.14 = bf16[2,16,1280]{2,0,1:T(2,128)(2,1)} copy(bf16[2,16,1280]{2,1,0:T(8,128)(2,1)S(1)} %convolution_convert_fusion.1) | data formatting | bytes 163840 | tf_op jit(solution)/shard_map/convert_element_type | solution.py:40
  12.7 7.4 %all-to-all-start = ((bf16[2,16,1280]{2,0,1:T(2,128)(2,1)}), bf16[2,16,1280]{2,0,1:T(2,128)(2,1)S(1)}, u32[]{:S(2)}, u32[]{:S(2)}) async-start(bf16[2,16,1280]{2,0,1:T(2,128)(2,1)} %copy.14), calls=%async_computation | async-start | bytes 163840 | tf_op jit(solution)/shard_map/all_to_all | solution.py:41
  20.1 0.0 reduce-scatter.2.cloned.1.call-start
  20.2 0.0 copy-done.2
  20.2 7.0 %all-to-all-done = bf16[2,16,1280]{2,0,1:T(2,128)(2,1)S(1)} async-done(((bf16[2,16,1280]{2,0,1:T(2,128)(2,1)}), bf16[2,16,1280]{2,0,1:T(2,128)(2,1)S(1)}, u32[]{:S(2)}, u32[]{:S(2)}) %all-to-all-start) | async-done | bytes 81952 | tf_op jit(solution)/shard_map/all_to_all | solution.py:41
  27.3 0.0 copy-start
  27.3 1.6 %collective-permute-start = (bf16[32,1,1280]{2,0,1:T(8,128)(2,1)S(1)}, bf16[32,1,1280]{2,0,1:T(8,128)(2,1)S(1)}, u32[]{:S(2)}, u32[]{:S(2)}) collective-permute-start(bf16[32,1,1280]{2,0,1:T(8,128)(2,1)S(1)} %all_to_all.29), channel_id=1, source_target_pairs={{0,1},{1,0},{2,3},{3,2},{4,5},{5,4},{6,7},{7,6},{8,9},{9,8},{10,11... | collective-permute-start | bytes 245768 | tf_op jit(solution)/shard_map/ppermute | solution.py:14
  28.9 3.2 %fusion.12 = f32[32,1,1792]{2,0,1:T(8,128)S(1)} fusion(bf16[32,1280]{1,0:T(8,128)(2,1)S(1)} %reshape.48, bf16[1,1280,1792]{2,1,0:T(8,128)(2,1)} %param.10), kind=kOutput, calls=%fused_computation.10 | convolution fusion | flops 146800640 | bytes 4898816 | tf_op jit(solution)/shard_map/rkd,kdf->rkf/dot_general | solution.py:48
  32.1 0.0 copy-start.4
  32.1 0.0 collective-permute-done
  32.1 0.0 copy-done
  32.1 0.9 %fusion.9 = f32[32,1,1792]{2,0,1:T(8,128)S(1)} fusion(bf16[1,1280,1792]{2,1,0:T(8,128)(2,1)S(1)} %copy-done, bf16[32,1,1280]{2,0,1:T(8,128)(2,1)S(1)} %collective-permute-done), kind=kOutput, calls=%fused_computation.9 | convolution fusion | flops 146800640 | bytes 4898816 | tf_op jit(solution)/shard_map/rkd,kdf->rkf/dot_general | solution.py:48
  33.0 1.4 %copy-done.4 = bf16[1,1792,1280]{2,1,0:T(8,128)(2,1)S(1)} copy-done((bf16[1,1792,1280]{2,1,0:T(8,128)(2,1)S(1)}, bf16[1,1792,1280]{2,1,0:T(8,128)(2,1)}, u32[]{:S(2)}) %copy-start.4) | copy-done | bytes 4587544
  34.4 0.0 copy-start.3
  34.4 1.8 %fusion.6 = f32[64,1,1280]{2,0,1:T(8,128)} fusion(bf16[1,1792,1280]{2,1,0:T(8,128)(2,1)S(1)} %copy-done.4, s32[]{:T(128)S(6)} %select_n.14, f32[32,1,1792]{2,0,1:T(8,128)S(1)} %fusion.9, f32[32,1,1792]{2,0,1:T(8,128)S(1)} %fusion.12, f32[1792]{0:T(1024)S(1)} %convert_reduce_fusion), kind=kOutput, calls=%fused_computation.8 | convolution fusion | flops 295092224 | bytes 5381124 | tf_op jit(solution)/shard_map/rkf,kfd->rkd/dot_general | solution.py:57
  36.2 0.0 reduce-scatter.2.cloned.1.call-update
  36.2 0.0 copy-done.3
  36.2 9.3 %reduce-scatter.2.cloned.1.call-done = f32[32,1,1280]{2,0,1:T(8,128)} async-done(((f32[64,1,1280]{2,0,1:T(8,128)}), f32[32,1,1280]{2,0,1:T(8,128)}) %reduce-scatter.2.cloned.1.call-update) | async-done | bytes 163856 | tf_op jit(solution)/shard_map/reduce_scatter | solution.py:56
  45.6 0.9 %add_convert_fusion = bf16[32,1,1280]{2,0,1:T(8,128)(2,1)S(1)} fusion(f32[32,1,1280]{2,0,1:T(8,128)} %reduce-scatter.2.cloned.1.call-done, f32[1280]{0:T(1024)S(1)} %convert_reduce_fusion.1), kind=kLoop, calls=%fused_computation.36 | loop fusion | flops 81920 | bytes 250880 | tf_op jit(solution)/shard_map/convert_element_type | solution.py:62
  46.5 0.5 broadcast.27
  47.0 0.7 reduce.5
  47.7 12.5 %all_to_all.36 = bf16[16,2,1280]{2,1,0:T(2,128)(2,1)S(1)} all-to-all(bf16[16,2,1280]{2,1,0:T(2,128)(2,1)S(1)} %reshape.57), channel_id=1, replica_groups=mesh['expert'=16,'tensor'=2] {'expert'}, dimensions={0} | all-to-all | bytes 163840 | tf_op jit(solution)/shard_map/all_to_all | solution.py:63
  60.3 0.1 reshape.58
  60.4 0.5 reduce.2
  60.9 1.6 %convolution_convert_fusion = bf16[2,256,1280]{2,1,0:T(8,128)(2,1)} fusion(bf16[16,2,1,1280]{3,1,0,2:T(2,128)(2,1)S(1)} %all_to_all.31, f32[2,256,16]{1,2,0:T(8,128)S(1)} %fusion.15), kind=kOutput, calls=%fused_computation.6 | convolution fusion | flops 21643792 | bytes 1425408 | tf_op jit(solution)/shard_map/ims,isd->imd/dot_general | solution.py:64
  (8 shorter events, 0.2 us)
Async XLA Ops:
  6.5 5.1 %copy-start.1 = (bf16[2,256,1280]{2,1,0:T(8,128)(2,1)S(1)}, bf16[2,256,1280]{2,1,0:T(8,128)(2,1)}, u32[]{:S(2)}) copy-start(bf16[2,256,1280]{2,1,0:T(8,128)(2,1)} %param.7) | copy-start | bytes 3932164
  6.5 13.7 %copy-start.2 = (bf16[1,1792]{1,0:T(2,128)(2,1)S(1)}, bf16[1,1792]{1,0:T(2,128)(2,1)}, u32[]{:S(2)}) copy-start(bf16[1,1792]{1,0:T(2,128)(2,1)} %param.11) | copy-start | bytes 10756
  12.7 14.5 %all-to-all-start = ((bf16[2,16,1280]{2,0,1:T(2,128)(2,1)}), bf16[2,16,1280]{2,0,1:T(2,128)(2,1)S(1)}, u32[]{:S(2)}, u32[]{:S(2)}) async-start(bf16[2,16,1280]{2,0,1:T(2,128)(2,1)} %copy.14), calls=%async_computation | async-start | bytes 163840 | tf_op jit(solution)/shard_map/all_to_all | solution.py:41
  20.1 25.4 %reduce-scatter.2.cloned.1.call-start = ((), (), s32[]{:S(2)}) async-start(), calls=%async_computation.3 | async-start | bytes 491520 | tf_op jit(solution)/shard_map/reduce_scatter | solution.py:56
  27.3 4.8 %copy-start = (bf16[1,1280,1792]{2,1,0:T(8,128)(2,1)S(1)}, bf16[1,1280,1792]{2,1,0:T(8,128)(2,1)}, u32[]{:S(2)}) copy-start(bf16[1,1280,1792]{2,1,0:T(8,128)(2,1)} %param.10) | copy-start | bytes 13762564
  27.3 4.8 %collective-permute-start = (bf16[32,1,1280]{2,0,1:T(8,128)(2,1)S(1)}, bf16[32,1,1280]{2,0,1:T(8,128)(2,1)S(1)}, u32[]{:S(2)}, u32[]{:S(2)}) collective-permute-start(bf16[32,1,1280]{2,0,1:T(8,128)(2,1)S(1)} %all_to_all.29), channel_id=1, source_target_pairs={{0,1},{1,0},{2,3},{3,2},{4,5},{5,4},{6,7},{7,6},{8,9},{9,8},{10,11... | collective-permute-start | bytes 245768 | tf_op jit(solution)/shard_map/ppermute | solution.py:14
  32.1 2.3 %copy-start.4 = (bf16[1,1792,1280]{2,1,0:T(8,128)(2,1)S(1)}, bf16[1,1792,1280]{2,1,0:T(8,128)(2,1)}, u32[]{:S(2)}) copy-start(bf16[1,1792,1280]{2,1,0:T(8,128)(2,1)} %param.12) | copy-start | bytes 13762564
  34.4 1.8 %copy-start.3 = (bf16[1,1280]{1,0:T(2,128)(2,1)S(1)}, bf16[1,1280]{1,0:T(2,128)(2,1)}, u32[]{:S(2)}) copy-start(bf16[1,1280]{1,0:T(2,128)(2,1)} %param.13) | copy-start | bytes 7684
Sparse Core Ops, SparseCore 0:
  36.3 9.2 reduce-scatter.1
